TPU v7x, 32 devices: a whole 2x2x4 slice. The times are simulated.
32 devices in a mesh: seq: 4 (over y, x), fsdp: 8 (over z, core).
Axes of the slice: x: 2, y: 2, z: 4, core: 2. Of those that a mesh axis runs over, the one named last changes fastest.
Arguments:
- tokens: bfloat16 [8, 512, 8192], P('fsdp', 'seq'), may hold values from -6 to 6
- norm_gain: float32 [8192], replicated, may hold values from 0.3 to 3
- w_query: bfloat16 [8192, 4096], P(('seq', 'fsdp')), may hold values from -1 to 1
- key_weight: bfloat16 [8192, 512], P(('seq', 'fsdp')), may hold values from -1 to 1
- value_weight: bfloat16 [8192, 512], P(('seq', 'fsdp')), may hold values from -0.0625 to 0.0625
- w_out: bfloat16 [4096, 8192], P(None, ('seq', 'fsdp')), may hold values from -0.09375 to 0.09375
Outputs:
- result: float32 [8, 512, 8192], P('fsdp', 'seq')
All inputs are finite; a program needn't handle non-finite values.
Results may differ from a plain program's by a relative error of at most 0.04.
Values may be sent and summed in bfloat16 or wider, within the bound.
A program may use at most 128 MiB of HBM per device.

v0:
```python
import jax
import jax.numpy as jnp
from jax import lax
from jax.sharding import PartitionSpec as P

HEAD_SIZE = 128


def body(tokens, norm_gain, w_query, key_weight, value_weight, w_out):
    floats = tokens[0].astype(jnp.float32)
    mean_square = jnp.mean(floats * floats, axis=-1, keepdims=True)
    normed_input = (floats * lax.rsqrt(mean_square + 1e-05) * norm_gain).astype(jnp.bfloat16)
    spread = lax.all_to_all(normed_input[None], "seq", split_axis=2, concat_axis=1, tiled=True)[0]
    seq_length = spread.shape[0]
    group_size = lax.axis_size("seq")
    device_index = lax.axis_index("seq")
    query_heads = w_query.shape[1] // HEAD_SIZE
    key_heads = key_weight.shape[1] // HEAD_SIZE
    group_width = query_heads // key_heads
    local_heads = query_heads // group_size
    portions = (
        lax.all_gather(w_query, "fsdp", axis=0, tiled=True),
        lax.all_gather(key_weight, "fsdp", axis=0, tiled=True),
        lax.all_gather(value_weight, "fsdp", axis=0, tiled=True),
    )
    query_part, key_part, value_part = tuple(
        (jnp.dot(spread, portion, preferred_element_type=jnp.float32) for portion in portions)
    )
    query_sum = lax.psum_scatter(
        query_part.astype(jnp.bfloat16), "seq", scatter_dimension=1, tiled=True
    )
    key_all, value_all = (
        lax.psum(key_part.astype(jnp.bfloat16), "seq").astype(jnp.float32),
        lax.psum(value_part.astype(jnp.bfloat16), "seq").astype(jnp.float32),
    )
    offset = device_index * local_heads // group_width * HEAD_SIZE
    key_rows = lax.dynamic_slice_in_dim(key_all, offset, HEAD_SIZE, 1).astype(jnp.bfloat16)
    value_rows = lax.dynamic_slice_in_dim(value_all, offset, HEAD_SIZE, 1).astype(jnp.bfloat16)
    queries = jnp.transpose(query_sum.reshape(seq_length, local_heads, HEAD_SIZE), (1, 0, 2))
    scale = HEAD_SIZE ** (-0.5)
    row_ids = lax.broadcasted_iota(jnp.int32, (seq_length, seq_length), 0)
    col_ids = lax.broadcasted_iota(jnp.int32, (seq_length, seq_length), 1)
    causal = row_ids >= col_ids

    def one_head(query_head):
        scores = (
            jnp.einsum("qd,kd->qk", query_head, key_rows, preferred_element_type=jnp.float32)
            * scale
        )
        scores = jnp.where(causal, scores, jnp.float32(-1e30))
        top = jnp.max(scores, axis=-1, keepdims=True)
        weights = jnp.exp(scores - top)
        probs = (weights / jnp.sum(weights, axis=-1, keepdims=True)).astype(jnp.bfloat16)
        return jnp.dot(probs, value_rows, preferred_element_type=jnp.float32).astype(jnp.bfloat16)

    attended = lax.map(one_head, queries)
    heads_out = jnp.transpose(attended, (1, 0, 2)).reshape(seq_length, local_heads * HEAD_SIZE)
    out_columns = lax.all_gather(w_out, "fsdp", axis=1, tiled=True)
    mixed = jnp.dot(
        lax.all_gather(heads_out, "seq", axis=1, tiled=True),
        out_columns,
        preferred_element_type=jnp.float32,
    )
    branch = mixed.astype(jnp.bfloat16)
    returned = lax.all_to_all(branch[None], "seq", split_axis=1, concat_axis=2, tiled=True)
    return tokens.astype(jnp.float32) + returned.astype(jnp.float32)


def solution(mesh):
    placed = (
        P("fsdp", "seq", None),
        P(),
        P(("seq", "fsdp"), None),
        P(("seq", "fsdp"), None),
        P(("seq", "fsdp"), None),
        P(None, ("seq", "fsdp")),
    )
    return jax.shard_map(
        body, mesh=mesh, in_specs=placed, out_specs=P("fsdp", "seq", None), check_vma=False
    )
```

profile of v0, /device:TPU:0, one launch (start us, length us, event | category | flops | bytes accessed | tf_op | source)
XLA Modules:
  0.0 635.2 jit_solution(5943152748968882074)
XLA Ops:
  9.3 1.9 fusion.10
  11.2 9.5 %copy.25 = bf16[1,128,8192]{1,0,2:T(2,128)(2,1)} copy(bf16[1,128,8192]{2,1,0:T(8,128)(2,1)} %fusion.10) | data formatting | bytes 4194304 | tf_op jit(solution)/shard_map/convert_element_type | solution.py:12
  21.3 46.5 %reduce.1 = bf16[8192,128]{1,0:T(8,128)(2,1)} reduce(bf16[8192,1,128]{2,1,0:T(2,128)(2,1)} %bitcast.52, bf16[]{:T(256)} %broadcast.27), dimensions={1}, to_apply=%bitcast.23.reduce_sub_computation | reduce | bytes 4194306
  67.8 4.0 reshape.53
  71.8 31.4 %all_to_all.24 = bf16[4,2,131072]{2,1,0:T(2,128)(2,1)} all-to-all(bf16[4,2,131072]{2,1,0:T(2,128)(2,1)} %reshape.53), channel_id=1, replica_groups=mesh['seq'=4,'fsdp'=8] {'seq'}, dimensions={0} | all-to-all | bytes 4194304 | tf_op jit(solution)/shard_map/all_to_all | solution.py:13
  103.2 4.9 reshape.54
  108.2 3.9 copy.33
  112.0 4.0 copy.26
  116.0 4.3 convolution_convert_fusion.3
  120.3 4.4 convolution_convert_fusion.4
  125.0 98.2 %all-gather.6.cloned.1.call-done = bf16[2048,4096]{1,0:T(8,128)(2,1)} async-done(((bf16[256,4096]{1,0:T(8,128)(2,1)}), bf16[2048,4096]{1,0:T(8,128)(2,1)}) %all-gather.6.cloned.1.call-update) | async-done | bytes 16777232 | tf_op jit(solution)/shard_map/all_gather | solution.py:22
  223.1 14.3 %convolution_convert_fusion.1 = bf16[512,4096]{1,0:T(8,128)(2,1)} fusion(bf16[512,2048]{1,0:T(8,128)(2,1)} %bitcast.60, bf16[2048,4096]{1,0:T(8,128)(2,1)} %all-gather.6.cloned.1.call-done), kind=kOutput, calls=%fused_computation.16 | convolution fusion | flops 8592031744 | bytes 23068672 | tf_op jit(solution)/shard_map/dot_general | solution.py:27
  238.1 38.6 %all-reduce.3.cloned.1.call-done = (bf16[512,512]{1,0:T(8,128)(2,1)}, bf16[512,512]{1,0:T(8,128)(2,1)}) async-done(((bf16[512,512]{1,0:T(8,128)(2,1)}, bf16[512,512]{1,0:T(8,128)(2,1)}), (bf16[512,512]{1,0:T(8,128)(2,1)}, bf16[512,512]{1,0:T(8,128)(2,1)})) %all-reduce.3.cloned.1.call-update) | async-done | bytes 1048592 | tf_op jit(solution)/shard_map/psum | solution.py:33
  276.8 1.6 convert_convert_fusion
  278.4 53.8 %reduce-scatter.2.cloned.1.call-done = bf16[512,1024]{1,0:T(8,128)(2,1)} async-done(((bf16[512,4096]{1,0:T(8,128)(2,1)}), bf16[512,1024]{1,0:T(8,128)(2,1)}) %reduce-scatter.2.cloned.1.call-update) | async-done | bytes 1048592 | tf_op jit(solution)/shard_map/reduce_scatter | solution.py:29
  332.2 2.4 bitcast_bitcast_fusion
  334.6 16.4 %while.11 = (s32[]{:T(128)}, bf16[8,512,128]{1,2,0:T(8,128)(2,1)S(1)}, bf16[8,512,128]{2,1,0:T(8,128)(2,1)}, bf16[512,128]{1,0:T(8,128)(2,1)}, bf16[512,128]{1,0:T(8,128)(2,1)S(1)}, /*index=5*/s32[]{:T(128)}) while((s32[]{:T(128)}, bf16[8,512,128]{1,2,0:T(8,128)(2,1)S(1)}, bf16[8,512,128]{2,1,0:T(8,128)(2,1)}, ...), condition=%wide.region_7.8_spmd.clone, body=%wide.region_4.7_spmd.clone.sunk | while | flops 136641536 | bytes 4205129 | solution.py:56
  340.6 1.3 fusion.31
  342.7 1.3 fusion.31
  344.8 1.3 fusion.31
  346.9 1.3 fusion.31
  351.9 133.5 %all-gather.14.cloned.1.call-done = bf16[4096,2048]{1,0:T(8,128)(2,1)} async-done(((bf16[4096,256]{1,0:T(8,128)(2,1)}), bf16[4096,2048]{1,0:T(8,128)(2,1)}) %all-gather.14.cloned.1.call-update) | async-done | bytes 16777232 | tf_op jit(solution)/shard_map/all_gather | solution.py:58
  485.5 52.6 %all-gather.12.cloned.1.call-done = bf16[512,4096]{0,1:T(8,128)(2,1)} async-done(((bf16[512,1024]{0,1:T(8,128)(2,1)}), bf16[512,4096]{0,1:T(8,128)(2,1)}) %all-gather.12.cloned.1.call-update) | async-done | bytes 4194320 | tf_op jit(solution)/shard_map/all_gather | solution.py:60
  538.1 13.6 %fusion.11 = bf16[1,512,2048]{2,1,0:T(8,128)(2,1)S(1)} fusion(bf16[512,4096]{0,1:T(8,128)(2,1)} %all-gather.12.cloned.1.call-done, bf16[4096,2048]{1,0:T(8,128)(2,1)} %all-gather.14.cloned.1.call-done), kind=kOutput, calls=%fused_computation.22 | convolution fusion | flops 8590983168 | bytes 23068672 | tf_op jit(solution)/shard_map/dot_general | solution.py:59
  551.7 5.2 copy.39
  557.0 14.5 %reduce.2 = bf16[512,2048]{1,0:T(8,128)(2,1)} reduce(bf16[512,1,2048]{2,1,0:T(2,128)(2,1)} %bitcast.53, bf16[]{:T(256)} %broadcast.27), dimensions={1}, to_apply=%bitcast.43.reduce_sub_computation | reduce | bytes 4194306
  571.5 4.5 reshape.55
  576.0 29.9 %all_to_all.25 = bf16[4,2,131072]{2,1,0:T(2,128)(2,1)} all-to-all(bf16[4,2,131072]{2,1,0:T(2,128)(2,1)} %reshape.55), channel_id=1, replica_groups=mesh['seq'=4,'fsdp'=8] {'seq'}, dimensions={0} | all-to-all | bytes 4194304 | tf_op jit(solution)/shard_map/all_to_all | solution.py:65
  605.9 4.9 reshape.56
  610.9 6.8 %copy.38 = f32[1,4,128,2048]{3,1,2,0:T(4,128)} copy(bf16[1,4,128,2048]{3,0,2,1:T(2,128)(2,1)} %bitcast.55) | data formatting | bytes 6291456 | tf_op jit(solution)/shard_map/convert_element_type | solution.py:66
  617.7 6.0 reshape.51
  623.7 4.6 convert_add_fusion
  (62 shorter events, 15.9 us)
Async XLA Ops:
  6.5 2.3 copy-start
  6.5 109.5 %all-gather.10.cloned.1.call-start = ((), (), s32[]{:S(2)}) async-start(), calls=%async_computation.6 | async-start | bytes 2359296 | tf_op jit(solution)/shard_map/all_gather | solution.py:24
  7.3 113.0 %all-gather.8.cloned.1.call-start = ((), (), s32[]{:S(2)}) async-start(), calls=%async_computation.5 | async-start | bytes 2359296 | tf_op jit(solution)/shard_map/all_gather | solution.py:23
  8.0 1.3 copy-start.2
  8.0 215.1 %all-gather.6.cloned.1.call-start = ((), (), s32[]{:S(2)}) async-start(), calls=%async_computation.3 | async-start | bytes 18874368 | tf_op jit(solution)/shard_map/all_gather | solution.py:22
  8.8 268.0 %all-reduce.3.cloned.1.call-start = ((), (), s32[]{:S(2)}) async-start(), calls=%async_computation.9 | async-start | bytes 2097152 | tf_op jit(solution)/shard_map/psum | solution.py:33
  124.7 207.4 %reduce-scatter.2.cloned.1.call-start = ((), (), s32[]{:S(2)}) async-start(), calls=%async_computation.4 | async-start | bytes 5242880 | tf_op jit(solution)/shard_map/reduce_scatter | solution.py:29
  237.5 248.0 %all-gather.14.cloned.1.call-start = ((), (), s32[]{:S(2)}) async-start(), calls=%async_computation.8 | async-start | bytes 18874368 | tf_op jit(solution)/shard_map/all_gather | solution.py:58
  238.0 300.0 %all-gather.12.cloned.1.call-start = ((), (), s32[]{:S(2)}) async-start(), calls=%async_computation.7 | async-start | bytes 5242880 | tf_op jit(solution)/shard_map/all_gather | solution.py:60
  350.9 1.0 copy-start.1
Sparse Core Ops, SparseCore 0:
  8.9 31.8 all-gather.9
  42.4 28.5 all-gather.7
  72.6 150.4 all-gather.5
  226.0 50.6 all-reduce.2
  279.6 52.5 reduce-scatter.1
  333.6 151.7 all-gather.13
  487.3 50.7 all-gather.11
where the time goes:
time: 636 us; the launch traced here: 635 us
  waiting for transfers between devices  379 us (60%)
  other arithmetic  71.3 us (11%)
  blocking collectives  61.3 us (10%)
  local copies, waits for them, and re-layouts  58.8 us (9%)
  matrix products  50.1 us (8%)
  between operations  13.6 us (2%)
    all_gather x1, waiting for transfers between devices, body(): out_columns = lax.all_gather(w_out, 'fsdp', axis=1, tiled=True)  134 us
    all_gather x1, waiting for transfers between devices, body(): lax.all_gather(w_query, 'fsdp', axis=0, tiled=True)  98.2 us
    unnamed x2, other arithmetic  61.1 us
    reduce_scatter x1, waiting for transfers between devices, body(): lax.psum_scatter(query_part.astype(jnp.bfloat16), 'seq', scatter_dimensio...  53.8 us
    all_gather x1, waiting for transfers between devices, body(): lax.all_gather(heads_out, 'seq', axis=1, tiled=True)  52.6 us
    psum x1, waiting for transfers between devices, body(): lax.psum(key_part.astype(jnp.bfloat16), 'seq').astype(jnp.float32)  38.6 us
    all_to_all x1, blocking collectives, body(): lax.all_to_all(normed_input[None], 'seq', split_axis=2, concat_axis=1, ti...  31.4 us
    all_to_all x1, blocking collectives, body(): lax.all_to_all(branch[None], 'seq', split_axis=1, concat_axis=2, tiled=True)  29.9 us
  transfers between devices with their start and end apart: 7, of which 5 were waited for; matrix products, arithmetic and copies ran while one was open for 19% of the time, Pallas kernels for 0%

commit v1 on v0

--- a/solution.py
+++ b/solution.py
@@ -4,6 +4,22 @@
 from jax.sharding import PartitionSpec as P
 
 HEAD_SIZE = 128
+
+
+def search_ports(obj):
+    width = lax.axis_size("fsdp")
+    grid = [(i, (i + 1) % width) for i in range(width)]
+
+    def _advance_indices(met_up):
+        if len(met_up) == width:
+            return met_up
+        val = _advance_indices([lax.ppermute(met_up[0], "fsdp", grid), *met_up])
+        return val
+
+    d_next = _advance_indices([obj])
+    field_out = jnp.concatenate(d_next, axis=1)
+    t_next = jnp.roll(field_out, (lax.axis_index("fsdp") + 1) * obj.shape[1], axis=1)
+    return t_next
 
 
 def body(tokens, norm_gain, w_query, key_weight, value_weight, w_out):
@@ -55,7 +71,7 @@
 
     attended = lax.map(one_head, queries)
     heads_out = jnp.transpose(attended, (1, 0, 2)).reshape(seq_length, local_heads * HEAD_SIZE)
-    out_columns = lax.all_gather(w_out, "fsdp", axis=1, tiled=True)
+    out_columns = search_ports(w_out)
     mixed = jnp.dot(
         lax.all_gather(heads_out, "seq", axis=1, tiled=True),
         out_columns,

time: 636 us -> 565 us (0.89)
  waiting for transfers between devices: 379 us -> 287 us
  local copies, waits for them, and re-layouts: 58.8 us -> 104 us
  blocking collectives: 61.3 us -> 29.9 us
    ppermute x0 -> x7, waiting for transfers between devices: none -> 149 us  [_advance_indices(): val = _advance_indices([lax.ppermute(met_up[0], 'fsdp', grid), *met_up])]
    all_gather x1 -> x0, waiting for transfers between devices: 134 us -> none  [body(): out_columns = lax.all_gather(w_out, 'fsdp', axis=1, tiled=True)]
    reduce_scatter x1, waiting for transfers between devices: 53.8 us -> 3.21 us  [body(): lax.psum_scatter(query_part.astype(jnp.bfloat16), 'seq', scatter_dimensio...]
    unnamed x12 -> x35, local copies, waits for them, and re-layouts: 23.8 us -> 67.2 us
    psum x1, waiting for transfers between devices: 38.6 us -> 0.01 us  [body(): lax.psum(key_part.astype(jnp.bfloat16), 'seq').astype(jnp.float32)]
    all_gather x1, waiting for transfers between devices: 52.6 us -> 16.7 us  [body(): lax.all_gather(heads_out, 'seq', axis=1, tiled=True)]
    all_to_all x1 -> x0, blocking collectives: 31.4 us -> none  [body(): lax.all_to_all(normed_input[None], 'seq', split_axis=2, concat_axis=1, ti...]
    all_to_all x0 -> x1, waiting for transfers between devices: none -> 25.3 us  [body(): lax.all_to_all(normed_input[None], 'seq', split_axis=2, concat_axis=1, ti...]
  transfers between devices with their start and end apart: 7 -> 14, of which waited for: 5 -> 9; matrix products, arithmetic and copies ran while one was open for 19% -> 26% of each run, Pallas kernels for 0% -> 0%
where the time goes in v1:
time: 565 us; the launch traced here: 563 us
  waiting for transfers between devices  287 us (51%)
  local copies, waits for them, and re-layouts  104 us (18%)
  other arithmetic  72.9 us (13%)
  matrix products  49.9 us (9%)
  blocking collectives  29.9 us (5%)
  between operations  13.6 us (2%)
  starting transfers between devices  5.89 us (1%)
    ppermute x7, waiting for transfers between devices, _advance_indices(): val = _advance_indices([lax.ppermute(met_up[0], 'fsdp', grid), *met_up])  149 us
    all_gather x1, waiting for transfers between devices, body(): lax.all_gather(w_query, 'fsdp', axis=0, tiled=True)  90.8 us
    unnamed x35, local copies, waits for them, and re-layouts  67.2 us
    unnamed x2, other arithmetic  61 us
    all_to_all x1, blocking collectives, body(): lax.all_to_all(branch[None], 'seq', split_axis=1, concat_axis=2, tiled=True)  29.9 us
    all_to_all x1, waiting for transfers between devices, body(): lax.all_to_all(normed_input[None], 'seq', split_axis=2, concat_axis=1, ti...  25.3 us
    dot_general x3, matrix products, body(): jnp.dot(spread, portion, preferred_element_type=jnp.float32)  23 us
    all_gather x1, waiting for transfers between devices, body(): lax.all_gather(heads_out, 'seq', axis=1, tiled=True)  16.7 us
  transfers between devices with their start and end apart: 14, of which 9 were waited for; matrix products, arithmetic and copies ran while one was open for 26% of the time, Pallas kernels for 0%

profile of v1, /device:TPU:0, one launch (start us, length us, event | category | flops | bytes accessed | tf_op | source)
XLA Modules:
  0.0 563.4 jit_solution(5845005740164583560)
XLA Ops:
  11.4 42.9 %collective-permute-done = bf16[4096,256]{1,0:T(8,128)(2,1)} collective-permute-done((bf16[4096,256]{1,0:T(8,128)(2,1)}, bf16[4096,256]{1,0:T(8,128)(2,1)}, u32[]{:S(2)}, u32[]{:S(2)}) %collective-permute-start) | collective-permute-done | bytes 2097184 | tf_op jit(solution)/shard_map/ppermute | solution.py:16
  56.2 9.5 %copy.25 = bf16[1,128,8192]{1,0,2:T(2,128)(2,1)} copy(bf16[1,128,8192]{2,1,0:T(8,128)(2,1)} %fusion.12) | data formatting | bytes 4194304 | tf_op jit(solution)/shard_map/convert_element_type | solution.py:28
  66.3 46.5 %reduce.1 = bf16[8192,128]{1,0:T(8,128)(2,1)} reduce(bf16[8192,1,128]{2,1,0:T(2,128)(2,1)} %bitcast.51, bf16[]{:T(256)} %broadcast.28), dimensions={1}, to_apply=%bitcast.23.reduce_sub_computation | reduce | bytes 4194306
  112.8 4.0 reshape.53
  116.8 4.5 all-to-all-start
  121.7 25.3 %all-to-all-done = bf16[4,2,131072]{2,1,0:T(2,128)(2,1)} async-done(((bf16[4,2,131072]{2,1,0:T(2,128)(2,1)}), bf16[4,2,131072]{2,1,0:T(2,128)(2,1)}, u32[]{:S(2)}, u32[]{:S(2)}) %all-to-all-start) | async-done | bytes 2097184 | tf_op jit(solution)/shard_map/all_to_all | solution.py:29
  147.0 4.9 reshape.54
  151.9 3.8 copy.33
  155.7 4.0 copy.26
  159.7 4.4 convolution_convert_fusion.2
  164.1 4.3 convolution_convert_fusion.3
  168.5 25.6 %collective-permute-done.2 = bf16[4096,256]{1,0:T(8,128)(2,1)} collective-permute-done((bf16[4096,256]{1,0:T(8,128)(2,1)}, bf16[4096,256]{1,0:T(8,128)(2,1)}, u32[]{:S(2)}, u32[]{:S(2)}) %collective-permute-start.2) | collective-permute-done | bytes 2097184 | tf_op jit(solution)/shard_map/ppermute | solution.py:16
  194.1 90.8 %all-gather.5.cloned.1.call-done = bf16[2048,4096]{1,0:T(8,128)(2,1)} async-done(((bf16[256,4096]{1,0:T(8,128)(2,1)}), bf16[2048,4096]{1,0:T(8,128)(2,1)}) %all-gather.5.cloned.1.call-update) | async-done | bytes 16777232 | tf_op jit(solution)/shard_map/all_gather | solution.py:38
  284.9 14.3 %convolution_convert_fusion.1 = bf16[512,4096]{1,0:T(8,128)(2,1)} fusion(bf16[512,2048]{1,0:T(8,128)(2,1)} %bitcast.59, bf16[2048,4096]{1,0:T(8,128)(2,1)} %all-gather.5.cloned.1.call-done), kind=kOutput, calls=%fused_computation.18 | convolution fusion | flops 8592031744 | bytes 23068672 | tf_op jit(solution)/shard_map/dot_general | solution.py:43
  299.6 27.2 %collective-permute-done.4 = bf16[4096,256]{1,0:T(8,128)(2,1)S(1)} collective-permute-done((bf16[4096,256]{1,0:T(8,128)(2,1)}, bf16[4096,256]{1,0:T(8,128)(2,1)S(1)}, u32[]{:S(2)}, u32[]{:S(2)}) %collective-permute-start.4) | collective-permute-done | bytes 2097184 | tf_op jit(solution)/shard_map/ppermute | solution.py:16
  328.2 27.4 %collective-permute-done.5 = bf16[4096,256]{1,0:T(8,128)(2,1)} collective-permute-done((bf16[4096,256]{1,0:T(8,128)(2,1)S(1)}, bf16[4096,256]{1,0:T(8,128)(2,1)}, u32[]{:S(2)}, u32[]{:S(2)}) %collective-permute-start.5) | collective-permute-done | bytes 2097184 | tf_op jit(solution)/shard_map/ppermute | solution.py:16
  357.2 25.9 %collective-permute-done.6 = bf16[4096,256]{1,0:T(8,128)(2,1)} collective-permute-done((bf16[4096,256]{1,0:T(8,128)(2,1)}, bf16[4096,256]{1,0:T(8,128)(2,1)}, u32[]{:S(2)}, u32[]{:S(2)}) %collective-permute-start.6) | collective-permute-done | bytes 2097184 | tf_op jit(solution)/shard_map/ppermute | solution.py:16
  390.8 3.2 reduce-scatter.2.cloned.1.call-done
  396.4 16.2 %while.11 = (s32[]{:T(128)}, bf16[8,512,128]{1,2,0:T(8,128)(2,1)S(1)}, bf16[8,512,128]{2,1,0:T(8,128)(2,1)}, bf16[512,128]{1,0:T(8,128)(2,1)}, bf16[512,128]{1,0:T(8,128)(2,1)S(1)}, /*index=5*/s32[]{:T(128)}) while((s32[]{:T(128)}, bf16[8,512,128]{1,2,0:T(8,128)(2,1)S(1)}, bf16[8,512,128]{2,1,0:T(8,128)(2,1)}, ...), condition=%wide.region_7.8_spmd.clone, body=%wide.region_4.7_spmd.clone.sunk | while | flops 136641536 | bytes 4204629 | solution.py:72
  419.8 3.5 constant_dynamic-update-slice_fusion.11
  427.9 3.2 constant_dynamic-update-slice_fusion.8
  441.8 3.2 constant_dynamic-update-slice_fusion.3
  449.6 16.7 %all-gather.11.cloned.1.call-done = bf16[512,4096]{0,1:T(8,128)(2,1)} async-done(((bf16[512,1024]{0,1:T(8,128)(2,1)}), bf16[512,4096]{0,1:T(8,128)(2,1)}) %all-gather.11.cloned.1.call-update) | async-done | bytes 4194320 | tf_op jit(solution)/shard_map/all_gather | solution.py:76
  466.3 13.6 %fusion.16 = bf16[1,512,2048]{2,1,0:T(8,128)(2,1)S(1)} fusion(bf16[512,4096]{0,1:T(8,128)(2,1)} %all-gather.11.cloned.1.call-done, bf16[4096,4096]{1,0:T(8,128)(2,1)} %constant_dynamic-update-slice_fusion.1, s32[]{:T(128)S(6)} %select_n.28), kind=kOutput, calls=%fused_computation.24 | convolution fusion | flops 8590983168 | bytes 23068676 | tf_op jit(solution)/shard_map/dot_general | solution.py:75
  479.9 5.2 copy.39
  485.2 14.5 %reduce.2 = bf16[512,2048]{1,0:T(8,128)(2,1)} reduce(bf16[512,1,2048]{2,1,0:T(2,128)(2,1)} %bitcast.52, bf16[]{:T(256)} %broadcast.28), dimensions={1}, to_apply=%bitcast.42.reduce_sub_computation | reduce | bytes 4194306
  499.7 4.5 reshape.55
  504.1 29.9 %all_to_all.24 = bf16[4,2,131072]{2,1,0:T(2,128)(2,1)} all-to-all(bf16[4,2,131072]{2,1,0:T(2,128)(2,1)} %reshape.55), channel_id=1, replica_groups=mesh['seq'=4,'fsdp'=8] {'seq'}, dimensions={0} | all-to-all | bytes 4194304 | tf_op jit(solution)/shard_map/all_to_all | solution.py:81
  534.1 4.9 reshape.56
  539.0 6.8 %copy.38 = f32[1,4,128,2048]{3,1,2,0:T(4,128)} copy(bf16[1,4,128,2048]{3,0,2,1:T(2,128)(2,1)} %bitcast.54) | data formatting | bytes 6291456 | tf_op jit(solution)/shard_map/convert_element_type | solution.py:82
  545.9 6.0 %reshape.51 = f32[1,128,8192]{2,1,0:T(8,128)} reshape(f32[1,128,4,2048]{3,2,1,0:T(4,128)} %bitcast.55) | data formatting | bytes 8388608 | tf_op jit(solution)/shard_map/convert_element_type | solution.py:82
  551.9 4.6 convert_add_fusion
  (98 shorter events, 64.1 us)
Async XLA Ops:
  6.5 47.7 %copy-start = (bf16[1,128,8192]{2,1,0:T(8,128)(2,1)S(1)}, bf16[1,128,8192]{2,1,0:T(8,128)(2,1)}, u32[]{:S(2)}) copy-start(bf16[1,128,8192]{2,1,0:T(8,128)(2,1)} %param.8) | copy-start | bytes 6291460
  6.5 47.7 %copy-start.6 = (f32[8192]{0:T(1024)S(1)}, f32[8192]{0:T(1024)}, u32[]{:S(2)}) copy-start(f32[8192]{0:T(1024)} %param.9) | copy-start | bytes 98308
  6.5 153.2 %all-gather.9.cloned.1.call-start = ((), (), s32[]{:S(2)}) async-start(), calls=%async_computation.6 | async-start | bytes 2359296 | tf_op jit(solution)/shard_map/all_gather | solution.py:40
  7.3 156.9 %all-gather.7.cloned.1.call-start = ((), (), s32[]{:S(2)}) async-start(), calls=%async_computation.5 | async-start | bytes 2359296 | tf_op jit(solution)/shard_map/all_gather | solution.py:39
  8.0 276.9 %all-gather.5.cloned.1.call-start = ((), (), s32[]{:S(2)}) async-start(), calls=%async_computation.3 | async-start | bytes 18874368 | tf_op jit(solution)/shard_map/all_gather | solution.py:38
  8.7 45.5 %collective-permute-start = (bf16[4096,256]{1,0:T(8,128)(2,1)}, bf16[4096,256]{1,0:T(8,128)(2,1)}, u32[]{:S(2)}, u32[]{:S(2)}) collective-permute-start(bf16[4096,256]{1,0:T(8,128)(2,1)} %param.13), channel_id=1, source_target_pairs={{0,1},{1,2},{2,3},{3,4},{4,5},{5,6},{6,7},{7,0},{8,9},{9,10},{10,1... | collective-permute-start | bytes 6291464 | tf_op jit(solution)/shard_map/ppermute | solution.py:16
  54.3 67.0 %collective-permute-start.1 = (bf16[4096,256]{1,0:T(8,128)(2,1)}, bf16[4096,256]{1,0:T(8,128)(2,1)}, u32[]{:S(2)}, u32[]{:S(2)}) collective-permute-start(bf16[4096,256]{1,0:T(8,128)(2,1)} %collective-permute-done), channel_id=1, source_target_pairs={{0,1},{1,2},{2,3},{3,4},{4,5},{5,6},{6,7},{7,0},{8,9},{9,10},{10,1... | collective-permute-start | bytes 6291464 | tf_op jit(solution)/shard_map/ppermute | solution.py:16
  116.8 30.2 %all-to-all-start = ((bf16[4,2,131072]{2,1,0:T(2,128)(2,1)}), bf16[4,2,131072]{2,1,0:T(2,128)(2,1)}, u32[]{:S(2)}, u32[]{:S(2)}) async-start(bf16[4,2,131072]{2,1,0:T(2,128)(2,1)} %reshape.53), calls=%async_computation | async-start | bytes 4194304 | tf_op jit(solution)/shard_map/all_to_all | solution.py:29
  121.3 234.3 %all-reduce.3.cloned.1.call-start = ((), (), s32[]{:S(2)}) async-start(), calls=%async_computation.8 | async-start | bytes 2097152 | tf_op jit(solution)/shard_map/psum | solution.py:49
  121.3 72.8 %collective-permute-start.2 = (bf16[4096,256]{1,0:T(8,128)(2,1)}, bf16[4096,256]{1,0:T(8,128)(2,1)}, u32[]{:S(2)}, u32[]{:S(2)}) collective-permute-start(bf16[4096,256]{1,0:T(8,128)(2,1)} %collective-permute-done.1), channel_id=1, source_target_pairs={{0,1},{1,2},{2,3},{3,4},{4,5},{5,6},{6,7},{7,0},{8,9},{9,10},{10,1... | collective-permute-start | bytes 6291464 | tf_op jit(solution)/shard_map/ppermute | solution.py:16
  168.4 225.6 %reduce-scatter.2.cloned.1.call-start = ((), (), s32[]{:S(2)}) async-start(), calls=%async_computation.4 | async-start | bytes 5242880 | tf_op jit(solution)/shard_map/reduce_scatter | solution.py:45
  194.1 105.2 %collective-permute-start.3 = (bf16[4096,256]{1,0:T(8,128)(2,1)}, bf16[4096,256]{1,0:T(8,128)(2,1)}, u32[]{:S(2)}, u32[]{:S(2)}) collective-permute-start(bf16[4096,256]{1,0:T(8,128)(2,1)} %collective-permute-done.2), channel_id=1, source_target_pairs={{0,1},{1,2},{2,3},{3,4},{4,5},{5,6},{6,7},{7,0},{8,9},{9,10},{10,1... | collective-permute-start | bytes 6291464 | tf_op jit(solution)/shard_map/ppermute | solution.py:16
  299.3 167.0 %all-gather.11.cloned.1.call-start = ((), (), s32[]{:S(2)}) async-start(), calls=%async_computation.7 | async-start | bytes 5242880 | tf_op jit(solution)/shard_map/all_gather | solution.py:76
  299.3 27.5 %collective-permute-start.4 = (bf16[4096,256]{1,0:T(8,128)(2,1)}, bf16[4096,256]{1,0:T(8,128)(2,1)S(1)}, u32[]{:S(2)}, u32[]{:S(2)}) collective-permute-start(bf16[4096,256]{1,0:T(8,128)(2,1)} %collective-permute-done.3), channel_id=1, source_target_pairs={{0,1},{1,2},{2,3},{3,4},{4,5},{5,6},{6,7},{7,0},{8,9},{9,10},{10,1... | collective-permute-start | bytes 6291464 | tf_op jit(solution)/shard_map/ppermute | solution.py:16
  326.8 1.4 copy-start.2
  328.2 27.4 %collective-permute-start.5 = (bf16[4096,256]{1,0:T(8,128)(2,1)S(1)}, bf16[4096,256]{1,0:T(8,128)(2,1)}, u32[]{:S(2)}, u32[]{:S(2)}) collective-permute-start(bf16[4096,256]{1,0:T(8,128)(2,1)S(1)} %collective-permute-done.4), channel_id=1, source_target_pairs={{0,1},{1,2},{2,3},{3,4},{4,5},{5,6},{6,7},{7,0},{8,9},{9,10},{10,1... | collective-permute-start | bytes 6291464 | tf_op jit(solution)/shard_map/ppermute | solution.py:16
  355.6 27.6 %collective-permute-start.6 = (bf16[4096,256]{1,0:T(8,128)(2,1)}, bf16[4096,256]{1,0:T(8,128)(2,1)}, u32[]{:S(2)}, u32[]{:S(2)}) collective-permute-start(bf16[4096,256]{1,0:T(8,128)(2,1)} %collective-permute-done.5), channel_id=1, source_target_pairs={{0,1},{1,2},{2,3},{3,4},{4,5},{5,6},{6,7},{7,0},{8,9},{9,10},{10,1... | collective-permute-start | bytes 6291464 | tf_op jit(solution)/shard_map/ppermute | solution.py:16
  357.2 32.1 %copy-start.3 = (bf16[4096,256]{1,0:T(8,128)(2,1)S(1)}, bf16[4096,256]{1,0:T(8,128)(2,1)}, u32[]{:S(2)}) copy-start(bf16[4096,256]{1,0:T(8,128)(2,1)} %copy-done.2) | copy-start | bytes 6291460
  412.6 1.0 copy-start.5
  419.8 6.6 %copy-start.1 = (bf16[4096,256]{1,0:T(8,128)(2,1)S(1)}, bf16[4096,256]{1,0:T(8,128)(2,1)}, u32[]{:S(2)}) copy-start(bf16[4096,256]{1,0:T(8,128)(2,1)} %param.13) | copy-start | bytes 6291460
  427.9 6.3 %copy-start.4 = (bf16[4096,256]{1,0:T(8,128)(2,1)S(1)}, bf16[4096,256]{1,0:T(8,128)(2,1)}, u32[]{:S(2)}) copy-start(bf16[4096,256]{1,0:T(8,128)(2,1)} %copy-done.2) | copy-start | bytes 6291460
Sparse Core Ops, SparseCore 0:
  8.9 41.6 all-gather.8
  52.2 37.1 all-gather.6
  91.0 193.8 all-gather.4
  287.8 50.6 all-reduce.2
  341.4 52.5 reduce-scatter.1
  413.7 52.5 all-gather.10
